TPU v7x, 512 devices: a whole 4x8x8 slice. The times are simulated.
512 devices in a mesh: dom: 64 (over x, y, core), grp: 8 (over z).
Axes of the slice: x: 4, y: 8, z: 8, core: 2. Of those that a mesh axis runs over, the one named last changes fastest.
Arguments:
- tangent_tiles: bfloat16 [65536, 128, 128], P(('grp', 'dom')), parts along dimension 0, may hold values from -0.5 to 0.5
- tile_blocks: int32 [8192, 2], P('dom'), may hold values from 0 to 511, as said below
- block_home: int32 [512], replicated, may hold values from 0 to 511, as said below
- tile_count: int32 [64], P('dom'), may hold values from 48 to 128, as said below
- basis: bfloat16 [65536, 256], P('dom'), may hold values from -0.29882812 to 0.29882812
Outputs:
- reduced: float32 [2048, 256], P('grp'), parts along dimension 0
There are 8 independent parts, one for each index of `grp`. A program takes and returns all parts, laid end to end along the dimension named above; an argument that names none is the same for every part. Nothing has to cross between parts.
Inputs may be any that keep to these rules, and one draw needn't show every extreme that they name: `tile_blocks`: every row block named by a device's tile slots has its position held by one of the devices with dom index from that device's index - 4 to its index + 8 // 2 - 1, taken cyclically. Among the row blocks named by one device's 128 slots, at most 2 distinct ones have their position held by any one device; every device reaches 2 for some holder. `block_home`: A permutation of the row blocks. `tile_count`: some device has exactly 128 live slots.
All inputs are finite; a program needn't handle non-finite values.
Results may differ from a plain program's by a relative error of at most 0.0029.
Values may be sent and summed in bfloat16 or wider, within the bound.
A program may use at most 64 MiB of HBM per device.

v0:
```python
import jax
import jax.numpy as jnp
from jax import lax
from jax.sharding import PartitionSpec as P

CAP = 2
NEAR = 8
GROUP = 16


def shifted(value, axis, steps):
    count = lax.axis_size(axis)
    pairs = [(source, (source + steps) % count) for source in range(count)]
    return lax.ppermute(value, axis, pairs)


def cut_along(x, dim, peers):
    dims = x.shape
    parts = x.reshape(*dims[:dim], peers, dims[dim] // peers, *dims[dim + 1 :])
    return jnp.moveaxis(parts, dim, 0)


def sent_and_summed(x, axis, dim):
    peers = lax.axis_size(axis)
    parts = lax.all_to_all(cut_along(x, dim, peers), axis, 0, 0, tiled=True)
    return jnp.sum(parts, axis=0)


def laid_out(parts, dim):
    parts = jnp.moveaxis(parts, 0, dim)
    dims = parts.shape
    return parts.reshape(*dims[:dim], dims[dim] * dims[dim + 1], *dims[dim + 2 :])


def sent_to_all(x, axis):
    copies = jnp.broadcast_to(x, (lax.axis_size(axis), *x.shape))
    return lax.all_to_all(copies, axis, split_axis=0, concat_axis=0, tiled=True)


def gather_directly(x, axis, dim):
    return laid_out(sent_to_all(x, axis), dim)


def on_device(tangent_tiles, tile_blocks, block_home, tile_count, basis):
    ndom = lax.axis_size("dom")
    tile_dev = tangent_tiles.shape[0]
    block = tangent_tiles.shape[1]
    rank = basis.shape[1]
    blk_dev = basis.shape[0] // block
    stored = basis.reshape(blk_dev, block, rank)
    place = jnp.take(block_home, tile_blocks.reshape(-1), axis=0)
    places = jnp.arange(ndom * blk_dev, dtype=jnp.int32)
    wanted = jnp.any(place[:, None] == places[None, :], axis=0).astype(jnp.int32)
    wanted = wanted.reshape(ndom, blk_dev)
    order = jnp.cumsum(wanted, axis=1) - 1
    levels = jnp.arange(CAP, dtype=jnp.int32)
    chosen = (wanted[:, :, None] == 1) & (order[:, :, None] == levels[None, None, :])
    local_ids = jnp.arange(blk_dev, dtype=jnp.int32)[None, :, None]
    requests = jnp.sum(jnp.where(chosen, local_ids, 0), axis=1)
    holder = place // blk_dev
    flat_order = order.reshape(-1)
    level_of = jnp.take(flat_order, place, axis=0)
    myself = lax.axis_index("dom")
    pieces = []
    for step_k in range(NEAR):
        away = step_k - NEAR // 2
        target = (myself + away) % ndom
        asking = lax.dynamic_index_in_dim(requests, target, 0, keepdims=False)
        if away == 0:
            pieces.append(jnp.take(stored, asking, axis=0))
        else:
            asked = shifted(asking, "dom", away)
            served = jnp.take(stored, asked, axis=0)
            pieces.append(shifted(served, "dom", -away))
    fetched = jnp.concatenate(pieces, axis=0)
    window_pos = (holder - myself + NEAR // 2) % ndom
    slot_of = window_pos * CAP + level_of
    slot_of = slot_of.reshape(tile_dev, 2)
    live = (jnp.arange(tile_dev, dtype=jnp.int32) < tile_count[0]).astype(jnp.float32)

    def project(step, total):
        begin = step * GROUP
        tile_set = lax.dynamic_slice_in_dim(tangent_tiles, begin, GROUP, 0)
        link_set = lax.dynamic_slice_in_dim(slot_of, begin, GROUP, 0)
        live_set = lax.dynamic_slice_in_dim(live, begin, GROUP, 0)
        cols = jnp.take(fetched, link_set[:, 1], axis=0)
        rows = jnp.take(fetched, link_set[:, 0], axis=0)
        right = jnp.einsum("tab,tbr->tar", tile_set, cols, preferred_element_type=jnp.float32)
        right = (right * live_set[:, None, None]).astype(jnp.bfloat16)
        return total + jnp.einsum(
            "ar,as->rs",
            rows.reshape(GROUP * block, rank),
            right.reshape(GROUP * block, rank),
            preferred_element_type=jnp.float32,
        )

    partial_sum = lax.fori_loop(0, tile_dev // GROUP, project, jnp.zeros((rank, rank), jnp.float32))
    own_rows = sent_and_summed(partial_sum, "dom", 0)
    reduced = gather_directly(own_rows, "dom", 0)
    return reduced


def solution(mesh):
    return jax.shard_map(
        on_device,
        mesh=mesh,
        in_specs=(P(("grp", "dom"), None, None), P("dom", None), P(), P("dom"), P("dom", None)),
        out_specs=P("grp", None),
        check_vma=False,
    )
```

profile of v0, /device:TPU:1, one launch (start us, length us, event | category | flops | bytes accessed | tf_op | source)
XLA Modules:
  0.0 156.5 jit_solution(16714414658275105504)
XLA Ops:
  4.0 5.6 %collective-permute-start.12 = (s32[2]{0:T(128)S(1)}, s32[2]{0:T(128)S(1)}, u32[]{:S(2)}, u32[]{:S(2)}) collective-permute-start(s32[2]{0:T(128)S(1)} %get-tuple-element.157), channel_id=1, source_target_pairs={{0,24},{8,32},{16,40},{24,48},{32,56},{40,64},{48,72},{56,80},{64,... | collective-permute-start | bytes 32 | tf_op jit(solution)/shard_map/ppermute | solution.py:14
  9.6 3.2 %collective-permute-start.10 = (s32[2]{0:T(128)S(1)}, s32[2]{0:T(128)S(1)}, u32[]{:S(2)}, u32[]{:S(2)}) collective-permute-start(s32[2]{0:T(128)S(1)} %get-tuple-element.158), channel_id=1, source_target_pairs={{0,16},{8,24},{16,32},{24,40},{32,48},{40,56},{48,64},{56,72},{64,... | collective-permute-start | bytes 32 | tf_op jit(solution)/shard_map/ppermute | solution.py:14
  12.8 2.2 %collective-permute-start.8 = (s32[2]{0:T(128)S(1)}, s32[2]{0:T(128)S(1)}, u32[]{:S(2)}, u32[]{:S(2)}) collective-permute-start(s32[2]{0:T(128)S(1)} %get-tuple-element.159), channel_id=1, source_target_pairs={{0,8},{8,16},{16,24},{24,32},{32,40},{40,48},{48,56},{56,64},{64,7... | collective-permute-start | bytes 32 | tf_op jit(solution)/shard_map/ppermute | solution.py:14
  15.0 3.5 %collective-permute-start.6 = (s32[2]{0:T(128)S(1)}, s32[2]{0:T(128)S(1)}, u32[]{:S(2)}, u32[]{:S(2)}) collective-permute-start(s32[2]{0:T(128)S(1)} %get-tuple-element.161), channel_id=1, source_target_pairs={{0,504},{8,0},{16,8},{24,16},{32,24},{40,32},{48,40},{56,48},{64,5... | collective-permute-start | bytes 32 | tf_op jit(solution)/shard_map/ppermute | solution.py:14
  18.5 7.0 %collective-permute-start.4 = (s32[2]{0:T(128)S(1)}, s32[2]{0:T(128)S(1)}, u32[]{:S(2)}, u32[]{:S(2)}) collective-permute-start(s32[2]{0:T(128)S(1)} %get-tuple-element.162), channel_id=1, source_target_pairs={{0,496},{8,504},{16,0},{24,8},{32,16},{40,24},{48,32},{56,40},{64,... | collective-permute-start | bytes 32 | tf_op jit(solution)/shard_map/ppermute | solution.py:14
  29.0 4.7 %collective-permute-start.2 = (s32[2]{0:T(128)S(1)}, s32[2]{0:T(128)S(1)}, u32[]{:S(2)}, u32[]{:S(2)}) collective-permute-start(s32[2]{0:T(128)S(1)} %get-tuple-element.163), channel_id=1, source_target_pairs={{0,488},{8,496},{16,504},{24,0},{32,8},{40,16},{48,24},{56,32},{64... | collective-permute-start | bytes 32 | tf_op jit(solution)/shard_map/ppermute | solution.py:14
  35.9 3.1 %collective-permute-done = s32[2]{0:T(128)S(1)} collective-permute-done((s32[2]{0:T(128)S(1)}, s32[2]{0:T(128)S(1)}, u32[]{:S(2)}, u32[]{:S(2)}) %collective-permute-start) | collective-permute-done | bytes 40 | tf_op jit(solution)/shard_map/ppermute | solution.py:14
  43.0 6.4 %collective-permute-start.13 = (bf16[2,128,256]{2,1,0:T(8,128)(2,1)S(1)}, bf16[2,128,256]{2,1,0:T(8,128)(2,1)S(1)}, u32[]{:S(2)}, u32[]{:S(2)}) collective-permute-start(bf16[2,128,256]{2,1,0:T(8,128)(2,1)S(1)} %broadcast_select_fusion), channel_id=1, source_target_pairs={{0,488},{8,496},{16,504},{24,0},{32,8},{40,16},{48,24},{56,32},{64... | collective-permute-start | bytes 393224 | tf_op jit(solution)/shard_map/ppermute | solution.py:14
  49.5 2.0 %collective-permute-start.11 = (bf16[2,128,256]{2,1,0:T(8,128)(2,1)S(1)}, bf16[2,128,256]{2,1,0:T(8,128)(2,1)S(1)}, u32[]{:S(2)}, u32[]{:S(2)}) collective-permute-start(bf16[2,128,256]{2,1,0:T(8,128)(2,1)S(1)} %broadcast_select_fusion.1), channel_id=1, source_target_pairs={{0,496},{8,504},{16,0},{24,8},{32,16},{40,24},{48,32},{56,40},{64,... | collective-permute-start | bytes 393224 | tf_op jit(solution)/shard_map/ppermute | solution.py:14
  51.7 2.2 %collective-permute-start.9 = (bf16[2,128,256]{2,1,0:T(8,128)(2,1)S(1)}, bf16[2,128,256]{2,1,0:T(8,128)(2,1)S(1)}, u32[]{:S(2)}, u32[]{:S(2)}) collective-permute-start(bf16[2,128,256]{2,1,0:T(8,128)(2,1)S(1)} %broadcast_select_fusion.2), channel_id=1, source_target_pairs={{0,504},{8,0},{16,8},{24,16},{32,24},{40,32},{48,40},{56,48},{64,5... | collective-permute-start | bytes 393224 | tf_op jit(solution)/shard_map/ppermute | solution.py:14
  54.0 4.4 %collective-permute-start.3 = (bf16[2,128,256]{2,1,0:T(8,128)(2,1)S(1)}, bf16[2,128,256]{2,1,0:T(8,128)(2,1)S(1)}, u32[]{:S(2)}, u32[]{:S(2)}) collective-permute-start(bf16[2,128,256]{2,1,0:T(8,128)(2,1)S(1)} %broadcast_select_fusion.5), channel_id=1, source_target_pairs={{0,24},{8,32},{16,40},{24,48},{32,56},{40,64},{48,72},{56,80},{64,... | collective-permute-start | bytes 393224 | tf_op jit(solution)/shard_map/ppermute | solution.py:14
  60.6 11.5 %collective-permute-done.1 = bf16[2,128,256]{2,1,0:T(8,128)(2,1)S(1)} collective-permute-done((bf16[2,128,256]{2,1,0:T(8,128)(2,1)S(1)}, bf16[2,128,256]{2,1,0:T(8,128)(2,1)S(1)}, u32[]{:S(2)}, u32[]{:S(2)}) %collective-permute-start.1) | collective-permute-done | bytes 131104 | tf_op jit(solution)/shard_map/ppermute | solution.py:14
  76.1 5.9 %collective-permute-done.5 = bf16[2,128,256]{2,1,0:T(8,128)(2,1)S(1)} collective-permute-done((bf16[2,128,256]{2,1,0:T(8,128)(2,1)S(1)}, bf16[2,128,256]{2,1,0:T(8,128)(2,1)S(1)}, u32[]{:S(2)}, u32[]{:S(2)}) %collective-permute-start.5) | collective-permute-done | bytes 131104 | tf_op jit(solution)/shard_map/ppermute | solution.py:14
  82.2 37.5 %while.14 = (s32[]{:T(128)}, f32[256,256]{1,0:T(8,128)S(1)}, s32[128,2]{0,1:T(2,128)S(1)}, bf16[16,128,256]{2,1,0:T(8,128)(2,1)S(1)}, bf16[128,128,128]{2,1,0:T(...) while((s32[]{:T(128)}, f32[256,256]{1,0:T(8,128)S(1)}, ...), condition=%wide.region_4.8_spmd.clone, body=%wide.region_3.7_spmd.clone.sunk | while | flops 404883648 | bytes 7349425 | solution.py:97
  84.7 2.3 %fusion.38 = f32[256,256]{1,0:T(8,128)S(1)} fusion(bf16[16,128,256]{2,1,0:T(8,128)(2,1)S(1)} %gather_fusion, bf16[16,128,256]{2,1,0:T(8,128)(2,1)} %gather_fusion.1, f32[16]{0:T(128)S(1)} %dynamic_slice.90, pred[16]{0:T(512)(128)(4,1)S(1)} %get-tuple-element.246, pred[16]{0:T(512)(128)(4,1)S(1)} %get-tuple-element.247, ...), kind=kOutput, calls=%fused_computation.15.clone.1 | convolution fusion | flops 404881408 | bytes 3145829 | tf_op jit(solution)/shard_map/while/body/eval_jaxpr/ar,as->rs/dot_general | solution.py:90
  89.3 2.3 %fusion.38 = f32[256,256]{1,0:T(8,128)S(1)} fusion(bf16[16,128,256]{2,1,0:T(8,128)(2,1)S(1)} %gather_fusion, bf16[16,128,256]{2,1,0:T(8,128)(2,1)} %gather_fusion.1, f32[16]{0:T(128)S(1)} %dynamic_slice.90, pred[16]{0:T(512)(128)(4,1)S(1)} %get-tuple-element.246, pred[16]{0:T(512)(128)(4,1)S(1)} %get-tuple-element.247, ...), kind=kOutput, calls=%fused_computation.15.clone.1 | convolution fusion | flops 404881408 | bytes 3145829 | tf_op jit(solution)/shard_map/while/body/eval_jaxpr/ar,as->rs/dot_general | solution.py:90
  94.0 2.3 %fusion.38 = f32[256,256]{1,0:T(8,128)S(1)} fusion(bf16[16,128,256]{2,1,0:T(8,128)(2,1)S(1)} %gather_fusion, bf16[16,128,256]{2,1,0:T(8,128)(2,1)} %gather_fusion.1, f32[16]{0:T(128)S(1)} %dynamic_slice.90, pred[16]{0:T(512)(128)(4,1)S(1)} %get-tuple-element.246, pred[16]{0:T(512)(128)(4,1)S(1)} %get-tuple-element.247, ...), kind=kOutput, calls=%fused_computation.15.clone.1 | convolution fusion | flops 404881408 | bytes 3145829 | tf_op jit(solution)/shard_map/while/body/eval_jaxpr/ar,as->rs/dot_general | solution.py:90
  98.7 2.3 %fusion.38 = f32[256,256]{1,0:T(8,128)S(1)} fusion(bf16[16,128,256]{2,1,0:T(8,128)(2,1)S(1)} %gather_fusion, bf16[16,128,256]{2,1,0:T(8,128)(2,1)} %gather_fusion.1, f32[16]{0:T(128)S(1)} %dynamic_slice.90, pred[16]{0:T(512)(128)(4,1)S(1)} %get-tuple-element.246, pred[16]{0:T(512)(128)(4,1)S(1)} %get-tuple-element.247, ...), kind=kOutput, calls=%fused_computation.15.clone.1 | convolution fusion | flops 404881408 | bytes 3145829 | tf_op jit(solution)/shard_map/while/body/eval_jaxpr/ar,as->rs/dot_general | solution.py:90
  103.4 2.3 %fusion.38 = f32[256,256]{1,0:T(8,128)S(1)} fusion(bf16[16,128,256]{2,1,0:T(8,128)(2,1)S(1)} %gather_fusion, bf16[16,128,256]{2,1,0:T(8,128)(2,1)} %gather_fusion.1, f32[16]{0:T(128)S(1)} %dynamic_slice.90, pred[16]{0:T(512)(128)(4,1)S(1)} %get-tuple-element.246, pred[16]{0:T(512)(128)(4,1)S(1)} %get-tuple-element.247, ...), kind=kOutput, calls=%fused_computation.15.clone.1 | convolution fusion | flops 404881408 | bytes 3145829 | tf_op jit(solution)/shard_map/while/body/eval_jaxpr/ar,as->rs/dot_general | solution.py:90
  108.1 2.3 %fusion.38 = f32[256,256]{1,0:T(8,128)S(1)} fusion(bf16[16,128,256]{2,1,0:T(8,128)(2,1)S(1)} %gather_fusion, bf16[16,128,256]{2,1,0:T(8,128)(2,1)} %gather_fusion.1, f32[16]{0:T(128)S(1)} %dynamic_slice.90, pred[16]{0:T(512)(128)(4,1)S(1)} %get-tuple-element.246, pred[16]{0:T(512)(128)(4,1)S(1)} %get-tuple-element.247, ...), kind=kOutput, calls=%fused_computation.15.clone.1 | convolution fusion | flops 404881408 | bytes 3145829 | tf_op jit(solution)/shard_map/while/body/eval_jaxpr/ar,as->rs/dot_general | solution.py:90
  112.8 2.3 %fusion.38 = f32[256,256]{1,0:T(8,128)S(1)} fusion(bf16[16,128,256]{2,1,0:T(8,128)(2,1)S(1)} %gather_fusion, bf16[16,128,256]{2,1,0:T(8,128)(2,1)} %gather_fusion.1, f32[16]{0:T(128)S(1)} %dynamic_slice.90, pred[16]{0:T(512)(128)(4,1)S(1)} %get-tuple-element.246, pred[16]{0:T(512)(128)(4,1)S(1)} %get-tuple-element.247, ...), kind=kOutput, calls=%fused_computation.15.clone.1 | convolution fusion | flops 404881408 | bytes 3145829 | tf_op jit(solution)/shard_map/while/body/eval_jaxpr/ar,as->rs/dot_general | solution.py:90
  117.5 2.3 %fusion.38 = f32[256,256]{1,0:T(8,128)S(1)} fusion(bf16[16,128,256]{2,1,0:T(8,128)(2,1)S(1)} %gather_fusion, bf16[16,128,256]{2,1,0:T(8,128)(2,1)} %gather_fusion.1, f32[16]{0:T(128)S(1)} %dynamic_slice.90, pred[16]{0:T(512)(128)(4,1)S(1)} %get-tuple-element.246, pred[16]{0:T(512)(128)(4,1)S(1)} %get-tuple-element.247, ...), kind=kOutput, calls=%fused_computation.15.clone.1 | convolution fusion | flops 404881408 | bytes 3145829 | tf_op jit(solution)/shard_map/while/body/eval_jaxpr/ar,as->rs/dot_general | solution.py:90
  119.8 17.9 %all_to_all.10 = f32[64,4,256]{2,1,0:T(4,128)S(1)} all-to-all(f32[64,4,256]{2,1,0:T(4,128)S(1)} %reshape.61), channel_id=1, replica_groups=mesh['dom'=64,'grp'=8] {'dom'}, dimensions={0} | all-to-all | bytes 524288 | tf_op jit(solution)/shard_map/all_to_all | solution.py:25
  137.8 17.9 %all_to_all.11 = f32[64,4,256]{2,1,0:T(4,128)S(1)} all-to-all(f32[64,4,256]{2,1,0:T(4,128)S(1)} %broadcast_in_dim.53), channel_id=1, replica_groups=mesh['dom'=64,'grp'=8] {'dom'}, dimensions={0} | all-to-all | bytes 524288 | tf_op jit(solution)/shard_map/all_to_all | solution.py:37
  (134 shorter events, 39.3 us)
Async XLA Ops:
  0.0 28.4 %copy-start = (bf16[1024,256]{1,0:T(8,128)(2,1)S(1)}, bf16[1024,256]{1,0:T(8,128)(2,1)}, u32[]{:S(2)}) copy-start(bf16[1024,256]{1,0:T(8,128)(2,1)} %param.17) | copy-start | bytes 1572868
  4.0 25.1 %collective-permute-start.12 = (s32[2]{0:T(128)S(1)}, s32[2]{0:T(128)S(1)}, u32[]{:S(2)}, u32[]{:S(2)}) collective-permute-start(s32[2]{0:T(128)S(1)} %get-tuple-element.157), channel_id=1, source_target_pairs={{0,24},{8,32},{16,40},{24,48},{32,56},{40,64},{48,72},{56,80},{64,... | collective-permute-start | bytes 32 | tf_op jit(solution)/shard_map/ppermute | solution.py:14
  9.6 24.2 %collective-permute-start.10 = (s32[2]{0:T(128)S(1)}, s32[2]{0:T(128)S(1)}, u32[]{:S(2)}, u32[]{:S(2)}) collective-permute-start(s32[2]{0:T(128)S(1)} %get-tuple-element.158), channel_id=1, source_target_pairs={{0,16},{8,24},{16,32},{24,40},{32,48},{40,56},{48,64},{56,72},{64,... | collective-permute-start | bytes 32 | tf_op jit(solution)/shard_map/ppermute | solution.py:14
  12.8 23.0 %collective-permute-start.8 = (s32[2]{0:T(128)S(1)}, s32[2]{0:T(128)S(1)}, u32[]{:S(2)}, u32[]{:S(2)}) collective-permute-start(s32[2]{0:T(128)S(1)} %get-tuple-element.159), channel_id=1, source_target_pairs={{0,8},{8,16},{16,24},{24,32},{32,40},{40,48},{48,56},{56,64},{64,7... | collective-permute-start | bytes 32 | tf_op jit(solution)/shard_map/ppermute | solution.py:14
  15.0 20.8 %collective-permute-start.6 = (s32[2]{0:T(128)S(1)}, s32[2]{0:T(128)S(1)}, u32[]{:S(2)}, u32[]{:S(2)}) collective-permute-start(s32[2]{0:T(128)S(1)} %get-tuple-element.161), channel_id=1, source_target_pairs={{0,504},{8,0},{16,8},{24,16},{32,24},{40,32},{48,40},{56,48},{64,5... | collective-permute-start | bytes 32 | tf_op jit(solution)/shard_map/ppermute | solution.py:14
  18.5 17.3 %collective-permute-start.4 = (s32[2]{0:T(128)S(1)}, s32[2]{0:T(128)S(1)}, u32[]{:S(2)}, u32[]{:S(2)}) collective-permute-start(s32[2]{0:T(128)S(1)} %get-tuple-element.162), channel_id=1, source_target_pairs={{0,496},{8,504},{16,0},{24,8},{32,16},{40,24},{48,32},{56,40},{64,... | collective-permute-start | bytes 32 | tf_op jit(solution)/shard_map/ppermute | solution.py:14
  29.0 6.8 %collective-permute-start.2 = (s32[2]{0:T(128)S(1)}, s32[2]{0:T(128)S(1)}, u32[]{:S(2)}, u32[]{:S(2)}) collective-permute-start(s32[2]{0:T(128)S(1)} %get-tuple-element.163), channel_id=1, source_target_pairs={{0,488},{8,496},{16,504},{24,0},{32,8},{40,16},{48,24},{56,32},{64... | collective-permute-start | bytes 32 | tf_op jit(solution)/shard_map/ppermute | solution.py:14
  33.8 5.2 %collective-permute-start = (s32[2]{0:T(128)S(1)}, s32[2]{0:T(128)S(1)}, u32[]{:S(2)}, u32[]{:S(2)}) collective-permute-start(s32[2]{0:T(128)S(1)} %get-tuple-element.164), channel_id=1, source_target_pairs={{0,480},{8,488},{16,496},{24,504},{32,0},{40,8},{48,16},{56,24},{6... | collective-permute-start | bytes 32 | tf_op jit(solution)/shard_map/ppermute | solution.py:14
  43.0 39.2 %collective-permute-start.13 = (bf16[2,128,256]{2,1,0:T(8,128)(2,1)S(1)}, bf16[2,128,256]{2,1,0:T(8,128)(2,1)S(1)}, u32[]{:S(2)}, u32[]{:S(2)}) collective-permute-start(bf16[2,128,256]{2,1,0:T(8,128)(2,1)S(1)} %broadcast_select_fusion), channel_id=1, source_target_pairs={{0,488},{8,496},{16,504},{24,0},{32,8},{40,16},{48,24},{56,32},{64... | collective-permute-start | bytes 393224 | tf_op jit(solution)/shard_map/ppermute | solution.py:14
  49.5 32.6 %collective-permute-start.11 = (bf16[2,128,256]{2,1,0:T(8,128)(2,1)S(1)}, bf16[2,128,256]{2,1,0:T(8,128)(2,1)S(1)}, u32[]{:S(2)}, u32[]{:S(2)}) collective-permute-start(bf16[2,128,256]{2,1,0:T(8,128)(2,1)S(1)} %broadcast_select_fusion.1), channel_id=1, source_target_pairs={{0,496},{8,504},{16,0},{24,8},{32,16},{40,24},{48,32},{56,40},{64,... | collective-permute-start | bytes 393224 | tf_op jit(solution)/shard_map/ppermute | solution.py:14
  51.7 30.5 %collective-permute-start.9 = (bf16[2,128,256]{2,1,0:T(8,128)(2,1)S(1)}, bf16[2,128,256]{2,1,0:T(8,128)(2,1)S(1)}, u32[]{:S(2)}, u32[]{:S(2)}) collective-permute-start(bf16[2,128,256]{2,1,0:T(8,128)(2,1)S(1)} %broadcast_select_fusion.2), channel_id=1, source_target_pairs={{0,504},{8,0},{16,8},{24,16},{32,24},{40,32},{48,40},{56,48},{64,5... | collective-permute-start | bytes 393224 | tf_op jit(solution)/shard_map/ppermute | solution.py:14
  54.0 20.1 %collective-permute-start.3 = (bf16[2,128,256]{2,1,0:T(8,128)(2,1)S(1)}, bf16[2,128,256]{2,1,0:T(8,128)(2,1)S(1)}, u32[]{:S(2)}, u32[]{:S(2)}) collective-permute-start(bf16[2,128,256]{2,1,0:T(8,128)(2,1)S(1)} %broadcast_select_fusion.5), channel_id=1, source_target_pairs={{0,24},{8,32},{16,40},{24,48},{32,56},{40,64},{48,72},{56,80},{64,... | collective-permute-start | bytes 393224 | tf_op jit(solution)/shard_map/ppermute | solution.py:14
  58.5 13.6 %collective-permute-start.1 = (bf16[2,128,256]{2,1,0:T(8,128)(2,1)S(1)}, bf16[2,128,256]{2,1,0:T(8,128)(2,1)S(1)}, u32[]{:S(2)}, u32[]{:S(2)}) collective-permute-start(bf16[2,128,256]{2,1,0:T(8,128)(2,1)S(1)} %broadcast_select_fusion.6), channel_id=1, source_target_pairs={{0,32},{8,40},{16,48},{24,56},{32,64},{40,72},{48,80},{56,88},{64,... | collective-permute-start | bytes 393224 | tf_op jit(solution)/shard_map/ppermute | solution.py:14
  72.1 9.9 %collective-permute-start.5 = (bf16[2,128,256]{2,1,0:T(8,128)(2,1)S(1)}, bf16[2,128,256]{2,1,0:T(8,128)(2,1)S(1)}, u32[]{:S(2)}, u32[]{:S(2)}) collective-permute-start(bf16[2,128,256]{2,1,0:T(8,128)(2,1)S(1)} %broadcast_select_fusion.4), channel_id=1, source_target_pairs={{0,16},{8,24},{16,32},{24,40},{32,48},{40,56},{48,64},{56,72},{64,... | collective-permute-start | bytes 393224 | tf_op jit(solution)/shard_map/ppermute | solution.py:14
  74.1 7.9 %collective-permute-start.7 = (bf16[2,128,256]{2,1,0:T(8,128)(2,1)S(1)}, bf16[2,128,256]{2,1,0:T(8,128)(2,1)S(1)}, u32[]{:S(2)}, u32[]{:S(2)}) collective-permute-start(bf16[2,128,256]{2,1,0:T(8,128)(2,1)S(1)} %broadcast_select_fusion.3), channel_id=1, source_target_pairs={{0,8},{8,16},{16,24},{24,32},{32,40},{40,48},{48,56},{56,64},{64,7... | collective-permute-start | bytes 393224 | tf_op jit(solution)/shard_map/ppermute | solution.py:14
where the time goes:
time: 157 us; the launch traced here: 156 us
  starting transfers between devices  49 us (31%)
  blocking collectives  35.7 us (23%)
  local copies, waits for them, and re-layouts  30.1 us (19%)
  waiting for transfers between devices  20.6 us (13%)
  matrix products  18 us (11%)
    ppermute x14, starting transfers between devices, shifted(): return lax.ppermute(value, axis, pairs)  49 us
    ppermute x14, waiting for transfers between devices, shifted(): return lax.ppermute(value, axis, pairs)  20.6 us
    dot_general x8, matrix products, project(): jnp.einsum('ar,as->rs', rows.reshape(GROUP * block, rank), right.reshape(...  18 us
    all_to_all x1, blocking collectives, sent_to_all(): return lax.all_to_all(copies, axis, split_axis=0, concat_axis=0, tiled=True)  17.9 us
    all_to_all x1, blocking collectives, sent_and_summed(): parts = lax.all_to_all(cut_along(x, dim, peers), axis, 0, 0, tiled=True)  17.9 us
    gather x8, local copies, waits for them, and re-layouts, project(): rows = jnp.take(fetched, link_set[:, 0], axis=0)  12.8 us
    gather x8, local copies, waits for them, and re-layouts, project(): cols = jnp.take(fetched, link_set[:, 1], axis=0)  4.91 us
    gather x7, local copies, waits for them, and re-layouts, on_device(): served = jnp.take(stored, asked, axis=0)  3.89 us
  transfers between devices with their start and end apart: 14, of which 3 were waited for; matrix products, arithmetic and copies ran while one was open for 2% of the time, Pallas kernels for 0%

commit v1 on v0

v1 whole, which is shorter than its diff:
```python
import functools

import jax
import jax.numpy as jnp
from jax import lax
from jax.experimental import pallas as pl
from jax.experimental.pallas import tpu as pltpu
from jax.sharding import PartitionSpec as P

NEAR = 8
HALF = NEAR // 2
ORDER = (2, 6, 3, 5, 1, 7, 0)
UNROLL = 8


def remote(src, dst, send, recv, where):
    return pltpu.make_async_remote_copy(
        src_ref=src,
        dst_ref=dst,
        send_sem=send,
        recv_sem=recv,
        device_id={"dom": where},
        device_id_type=pl.DeviceIdType.MESH,
    )


def kernel(
    ndom,
    links_ref,
    home_ref,
    count_ref,
    tiles_hbm,
    basis_hbm,
    out_ref,
    tiles,
    stored,
    req_out,
    req_in,
    serve,
    fetched,
    turned,
    slots_v,
    slots,
    total,
    parts,
    came,
    final,
    tile_sem,
    basis_sem,
    slot_sem,
    req_send,
    req_recv,
    blk_send,
    blk_recv,
    sum_send,
    sum_recv,
    all_send,
    all_recv,
):
    me = lax.axis_index("dom")
    mask = ndom - 1

    basis_copy = pltpu.make_async_copy(basis_hbm, stored, basis_sem)
    basis_copy.start()
    tile_copy = pltpu.make_async_copy(tiles_hbm, tiles, tile_sem)
    tile_copy.start()

    barrier = pltpu.get_barrier_semaphore()

    def greet(k, carry):
        other = (me + k) & mask
        pl.semaphore_signal(barrier, inc=1, device_id={"dom": other}, device_id_type=pl.DeviceIdType.MESH)
        return carry

    lax.fori_loop(1, ndom, greet, 0)

    sub = lax.broadcasted_iota(jnp.int32, (8, 128), 0)

    def looked_up(row):
        ids = jnp.broadcast_to(links_ref[row : row + 1, :], (8, 128))
        place = jnp.zeros((8, 128), jnp.int32)
        for k in range(home_ref.shape[0]):
            table = jnp.broadcast_to(home_ref[k : k + 1, :], (8, 128))
            got = jnp.take_along_axis(table, ids & 127, axis=1)
            place = jnp.where((ids >> 7) == k, got, place)
        window = ((place >> 3) - me + HALF + ndom) & mask
        return window, place & 7, window == sub

    row_win, row_id, row_hit = looked_up(0)
    col_win, col_id, col_hit = looked_up(1)
    low = jnp.minimum(jnp.where(row_hit, row_id, 7), jnp.where(col_hit, col_id, 7))
    high = jnp.maximum(jnp.where(row_hit, row_id, 0), jnp.where(col_hit, col_id, 0))
    low = jnp.broadcast_to(jnp.min(low, axis=1, keepdims=True), (8, 128))
    high = jnp.broadcast_to(jnp.max(high, axis=1, keepdims=True), (8, 128))
    packed = low + 16 * high
    for w in range(NEAR):
        req_out[w] = jnp.broadcast_to(packed[w : w + 1, :], (8, 128))

    def slot_of(window, ids, hit):
        level = jnp.sum(jnp.where(hit & (ids != low), 1, 0), axis=0, keepdims=True)
        return jnp.minimum(2 * window[0:1] + level, 2 * NEAR - 1)

    row_slot = slot_of(row_win, row_id, row_hit)
    col_slot = slot_of(col_win, col_id, col_hit)
    lane = lax.broadcasted_iota(jnp.int32, (1, 128), 1)
    col_slot = jnp.where(lane < count_ref[0], col_slot, 2 * NEAR)
    slots_v[0:1, :] = row_slot
    slots_v[1:2, :] = col_slot
    slot_copy = pltpu.make_async_copy(slots_v, slots, slot_sem)
    slot_copy.start()

    pl.semaphore_wait(barrier, ndom - 1)

    def holder_of(w):
        return (me + (w - HALF + ndom)) & mask

    def asker_of(w):
        return (me + (HALF - w + ndom)) & mask

    for w in ORDER:
        remote(req_out.at[w], req_in.at[w], req_send.at[w], req_recv.at[w], holder_of(w)).start()

    basis_copy.wait()
    own = packed[HALF, 0]
    fetched[2 * HALF] = stored[own & 7]
    fetched[2 * HALF + 1] = stored[(own >> 4) & 7]
    fetched[2 * NEAR] = jnp.zeros(fetched.shape[1:], fetched.dtype)

    for w in ORDER:
        remote(req_out.at[w], req_in.at[w], req_send.at[w], req_recv.at[w], asker_of(w)).wait_recv()
        asked = req_in[w, 0, 0]
        serve[w, 0] = stored[asked & 7]
        serve[w, 1] = stored[(asked >> 4) & 7]
        remote(serve.at[w], fetched.at[pl.ds(2 * w, 2)], blk_send.at[w], blk_recv.at[w], asker_of(w)).start()

    for w in (HALF,) + ORDER:
        if w != HALF:
            remote(serve.at[w], fetched.at[pl.ds(2 * w, 2)], blk_send.at[w], blk_recv.at[w], holder_of(w)).wait_recv()
        turned[2 * w] = fetched[2 * w].T
        turned[2 * w + 1] = fetched[2 * w + 1].T

    slot_copy.wait()
    tile_copy.wait()
    total[...] = jnp.zeros_like(total)

    def project(step, carry):
        lefts, rights = [], []
        for u in range(UNROLL):
            t = step * UNROLL + u
            right = jnp.dot(tiles[t], fetched[slots[1, t]], preferred_element_type=jnp.float32)
            rights.append(right.astype(jnp.bfloat16))
            lefts.append(turned[slots[0, t]])
        total[...] += jnp.dot(
            jnp.concatenate(lefts, axis=1), jnp.concatenate(rights, axis=0), preferred_element_type=jnp.float32
        )
        return carry

    lax.fori_loop(0, tiles.shape[0] // UNROLL, project, 0)

    def cut(g, carry):
        rows = total[pl.ds(pl.multiple_of(g * 8, 8), 8), :].astype(jnp.bfloat16)
        parts[2 * g] = rows[:, :128]
        parts[2 * g + 1] = rows[:, 128:]
        return carry

    lax.fori_loop(0, ndom // 2, cut, 0)

    def send_part(k, carry):
        other = (me + k) & mask
        remote(parts.at[other], came.at[me], sum_send, sum_recv, other).start()
        return carry

    lax.fori_loop(1, ndom, send_part, 0)
    came[me] = parts[me]
    others = pl.ds(0, ndom - 1)
    remote(came.at[others], came.at[others], sum_send, sum_recv, me).wait_recv()
    summed = jnp.sum(came[...].astype(jnp.float32), axis=0)
    final[me] = summed.astype(jnp.bfloat16)

    def send_sum(k, carry):
        other = (me + k) & mask
        remote(final.at[me], final.at[me], all_send, all_recv, other).start()
        return carry

    lax.fori_loop(1, ndom, send_sum, 0)
    remote(final.at[others], final.at[others], all_send, all_recv, me).wait_recv()

    def put(g, carry):
        at = pl.ds(pl.multiple_of(g * 8, 8), 8)
        out_ref[at, 0:128] = final[2 * g].astype(jnp.float32)
        out_ref[at, 128:256] = final[2 * g + 1].astype(jnp.float32)
        return carry

    lax.fori_loop(0, ndom // 2, put, 0)

    for w in ORDER:
        remote(req_out.at[w], req_in.at[w], req_send.at[w], req_recv.at[w], holder_of(w)).wait_send()
        remote(serve.at[w], fetched.at[pl.ds(2 * w, 2)], blk_send.at[w], blk_recv.at[w], asker_of(w)).wait_send()
    remote(parts.at[others], parts.at[others], sum_send, sum_recv, me).wait_send()
    remote(final.at[others], final.at[others], all_send, all_recv, me).wait_send()


def solution(mesh):
    ndom = mesh.shape["dom"]

    def on_device(tangent_tiles, tile_blocks, block_home, tile_count, basis):
        count, block = tangent_tiles.shape[:2]
        rank = basis.shape[1]
        held = basis.shape[0] // block
        bf16, f32, i32 = jnp.bfloat16, jnp.float32, jnp.int32
        vmem, dma = pltpu.VMEM, pltpu.SemaphoreType.DMA
        return pl.pallas_call(
            functools.partial(kernel, ndom),
            out_shape=jax.ShapeDtypeStruct((rank, rank), f32),
            in_specs=[
                pl.BlockSpec(memory_space=pltpu.VMEM),
                pl.BlockSpec(memory_space=pltpu.VMEM),
                pl.BlockSpec(memory_space=pltpu.SMEM),
                pl.BlockSpec(memory_space=pl.ANY),
                pl.BlockSpec(memory_space=pl.ANY),
            ],
            out_specs=pl.BlockSpec(memory_space=pltpu.VMEM),
            scratch_shapes=[
                vmem((count, block, block), bf16),
                vmem((held, block, rank), bf16),
                vmem((NEAR, 8, 128), i32),
                vmem((NEAR, 8, 128), i32),
                vmem((NEAR, 2, block, rank), bf16),
                vmem((2 * NEAR + 1, block, rank), bf16),
                vmem((2 * NEAR, rank, block), bf16),
                vmem((2, 128), i32),
                pltpu.SMEM((2, 128), i32),
                vmem((rank, rank), f32),
                vmem((ndom, 8, 128), bf16),
                vmem((ndom, 8, 128), bf16),
                vmem((ndom, 8, 128), bf16),
                dma,
                dma,
                dma,
                dma((NEAR,)),
                dma((NEAR,)),
                dma((NEAR,)),
                dma((NEAR,)),
                dma,
                dma,
                dma,
                dma,
            ],
            compiler_params=pltpu.CompilerParams(
                collective_id=0, has_side_effects=True
            ),
        )(
            tile_blocks.T,
            block_home.reshape(-1, 128),
            tile_count,
            tangent_tiles,
            basis.reshape(held, block, rank),
        )

    return jax.shard_map(
        on_device,
        mesh=mesh,
        in_specs=(P(("grp", "dom"), None, None), P("dom", None), P(), P("dom"), P("dom", None)),
        out_specs=P("grp", None),
        check_vma=False,
    )
```

time: 157 us -> 58.1 us (0.37)
  Pallas kernels: 0 us -> 55.6 us
  starting transfers between devices: 49 us -> 0 us
  blocking collectives: 35.7 us -> 0 us
  local copies, waits for them, and re-layouts: 30.1 us -> 1.67 us
  waiting for transfers between devices: 20.6 us -> 0 us
  matrix products: 18 us -> 0 us
    pallas_call x0 -> x1, Pallas kernels: none -> 55.6 us  [on_device(): pl.pallas_call(functools.partial(kernel, ndom), out_shape=jax.ShapeDtypeS...]
    ppermute x14 -> x0, starting transfers between devices: 49 us -> none  [shifted(): return lax.ppermute(value, axis, pairs)]
    all_to_all x2 -> x0, blocking collectives: 35.7 us -> none  [the longest x1 17.9 us: sent_to_all(): return lax.all_to_all(copies, axis, split_axis=0, concat_axis=0, tiled=True)]
    gather x26 -> x0, local copies, waits for them, and re-layouts: 26.1 us -> none  [the longest x8 12.8 us: project(): rows = jnp.take(fetched, link_set[:, 0], axis=0)]
    ppermute x14 -> x0, waiting for transfers between devices: 20.6 us -> none  [shifted(): return lax.ppermute(value, axis, pairs)]
    dot_general x8 -> x0, matrix products: 18 us -> none  [project(): jnp.einsum('ar,as->rs', rows.reshape(GROUP * block, rank), right.reshape(...]
  transfers between devices with their start and end apart: 14 -> 0, of which waited for: 3 -> 0; matrix products, arithmetic and copies ran while one was open for 2% -> 0% of each run, Pallas kernels for 0% -> 0%
where the time goes in v1:
time: 58.1 us; the launch traced here: 57.9 us
  Pallas kernels  55.6 us (96%)
  local copies, waits for them, and re-layouts  1.67 us (3%)
  between operations  0.66 us (1%)
    pallas_call x1, Pallas kernels, on_device(): pl.pallas_call(functools.partial(kernel, ndom), out_shape=jax.ShapeDtypeS...  55.6 us
    unnamed x1, local copies, waits for them, and re-layouts  1.67 us

profile of v1, /device:TPU:1, one launch (start us, length us, event | category | flops | bytes accessed | tf_op | source)
XLA Modules:
  0.0 57.9 jit_solution(15073679959380046049)
XLA Ops:
  0.7 55.6 %shard_map.55 = f32[256,256]{1,0:T(8,128)} custom-call(s32[2,128]{1,0:T(2,128)} %bitcast.5, s32[4,128]{1,0:T(4,128)} %bitcast.4, s32[1]{0:T(128)S(6)} %copy.7.count_ref, bf16[128,128,128]{2,1,0:T(8,128)(2,1)} %tiles_hbm.1, bf16[8,128,256]{2,1,0:T(8,128)(2,1)} %bitcast.3), custom_call_target="tpu_custom_call" | custom-call | tf_op jit(solution)/shard_map/pallas_call | solution.py:212
  56.2 1.7 %copy.8 = f32[256,256]{1,0:T(8,128)} copy(f32[256,256]{1,0:T(8,128)} %shard_map.55) | data formatting | bytes 524288

commit v2 on v1

--- a/solution.py
+++ b/solution.py
@@ -9,8 +9,10 @@
 
 NEAR = 8
 HALF = NEAR // 2
-ORDER = (2, 6, 3, 5, 1, 7, 0)
+DIRECT = (2, 6, 3, 5)
 UNROLL = 8
+TEAM = 4
+GRP = 8
 
 
 def remote(src, dst, send, recv, where):
@@ -19,9 +21,20 @@
         dst_ref=dst,
         send_sem=send,
         recv_sem=recv,
-        device_id={"dom": where},
+        device_id=where,
         device_id_type=pl.DeviceIdType.MESH,
     )
+
+
+def signal(sem, where):
+    pl.semaphore_signal(sem, inc=1, device_id=where, device_id_type=pl.DeviceIdType.MESH)
+
+
+def team_of(depth, team):
+    place = (depth + 2 * team) & (TEAM - 1)
+    first = depth - place + GRP
+    others = [(first + ((place + k) & (TEAM - 1))) & (GRP - 1) for k in range(1, TEAM)]
+    return place, others
 
 
 def kernel(
@@ -37,6 +50,7 @@
     req_out,
     req_in,
     serve,
+    serve_part,
     fetched,
     turned,
     slots_v,
@@ -52,13 +66,20 @@
     req_recv,
     blk_send,
     blk_recv,
+    far_send,
+    far_recv,
+    pass_send,
+    pass_recv,
+    round_sem,
     sum_send,
     sum_recv,
     all_send,
     all_recv,
 ):
     me = lax.axis_index("dom")
+    depth = lax.axis_index("grp")
     mask = ndom - 1
+    core = me & 1
 
     basis_copy = pltpu.make_async_copy(basis_hbm, stored, basis_sem)
     basis_copy.start()
@@ -66,13 +87,12 @@
     tile_copy.start()
 
     barrier = pltpu.get_barrier_semaphore()
-
-    def greet(k, carry):
-        other = (me + k) & mask
-        pl.semaphore_signal(barrier, inc=1, device_id={"dom": other}, device_id_type=pl.DeviceIdType.MESH)
-        return carry
-
-    lax.fori_loop(1, ndom, greet, 0)
+    for step in range(1, HALF + 1):
+        for other in ((me + step) & mask, (me - step + ndom) & mask):
+            signal(barrier, {"dom": other})
+    for team in (0, 1):
+        for other in team_of(depth, team)[1]:
+            signal(barrier, {"grp": other})
 
     sub = lax.broadcasted_iota(jnp.int32, (8, 128), 0)
 
@@ -109,7 +129,7 @@
     slot_copy = pltpu.make_async_copy(slots_v, slots, slot_sem)
     slot_copy.start()
 
-    pl.semaphore_wait(barrier, ndom - 1)
+    pl.semaphore_wait(barrier, 2 * HALF + 2 * (TEAM - 1))
 
     def holder_of(w):
         return (me + (w - HALF + ndom)) & mask
@@ -117,8 +137,36 @@
     def asker_of(w):
         return (me + (HALF - w + ndom)) & mask
 
-    for w in ORDER:
-        remote(req_out.at[w], req_in.at[w], req_send.at[w], req_recv.at[w], holder_of(w)).start()
+    rows_far = fetched.shape[1] // TEAM
+    ask_far = (0, 1 + 6 * core)
+    ask_near = DIRECT + (7 - 6 * core,)
+    serve_far = (0, 7 - 6 * core)
+    serve_near = DIRECT + (1 + 6 * core,)
+
+    def share(ref, w, team, place):
+        at = pl.ds(pl.multiple_of(place * rows_far, rows_far), rows_far)
+        return ref.at[pl.ds(2 * w, 2), at]
+
+    def request(w, where):
+        return remote(req_out.at[w], req_in.at[w], req_send.at[w], req_recv.at[w], {"dom": where})
+
+    def far(n, w, where):
+        place = team_of(depth, n)[0]
+        part = share(fetched, w, n, place)
+        return remote(serve_part.at[n], part, far_send.at[n], far_recv.at[n], {"dom": where})
+
+    def near(n, w, where):
+        return remote(serve.at[n], fetched.at[pl.ds(2 * w, 2)], blk_send.at[n], blk_recv.at[n], {"dom": where})
+
+    def pass_on(n, w, k):
+        place, others = team_of(depth, n)
+        part = share(fetched, w, n, place)
+        return remote(part, part, pass_send.at[n, k], pass_recv.at[n], {"grp": others[k]})
+
+    for w in ask_far + ask_near:
+        request(w, holder_of(w)).start()
+    for other in ((me + HALF) & mask, (me - HALF + ndom) & mask):
+        signal(round_sem.at[0], {"dom": other})
 
     basis_copy.wait()
     own = packed[HALF, 0]
@@ -126,18 +174,45 @@
     fetched[2 * HALF + 1] = stored[(own >> 4) & 7]
     fetched[2 * NEAR] = jnp.zeros(fetched.shape[1:], fetched.dtype)
 
-    for w in ORDER:
-        remote(req_out.at[w], req_in.at[w], req_send.at[w], req_recv.at[w], asker_of(w)).wait_recv()
+    for n, w in enumerate(serve_far):
+        request(w, asker_of(w)).wait_recv()
         asked = req_in[w, 0, 0]
-        serve[w, 0] = stored[asked & 7]
-        serve[w, 1] = stored[(asked >> 4) & 7]
-        remote(serve.at[w], fetched.at[pl.ds(2 * w, 2)], blk_send.at[w], blk_recv.at[w], asker_of(w)).start()
-
-    for w in (HALF,) + ORDER:
-        if w != HALF:
-            remote(serve.at[w], fetched.at[pl.ds(2 * w, 2)], blk_send.at[w], blk_recv.at[w], holder_of(w)).wait_recv()
+        at = pl.ds(pl.multiple_of(team_of(depth, n)[0] * rows_far, rows_far), rows_far)
+        serve_part[n, 0] = stored[asked & 7, at]
+        serve_part[n, 1] = stored[(asked >> 4) & 7, at]
+        far(n, w, asker_of(w)).start()
+    for n, w in enumerate(serve_near):
+        request(w, asker_of(w)).wait_recv()
+        asked = req_in[w, 0, 0]
+        serve[n, 0] = stored[asked & 7]
+        serve[n, 1] = stored[(asked >> 4) & 7]
+        near(n, w, asker_of(w)).start()
+
+    def meet(n, gap):
+        pl.semaphore_wait(round_sem.at[n], 2)
+        for other in ((me + gap) & mask, (me - gap + ndom) & mask):
+            signal(round_sem.at[n + 1], {"dom": other})
+
+    meet(0, 2 * HALF)
+    for n, w in enumerate(ask_far):
+        far(n, w, holder_of(w)).wait_recv()
+        for k in range(TEAM - 1):
+            pass_on(n, w, k).start()
+    meet(1, 4 * HALF)
+
+    def turn(w):
         turned[2 * w] = fetched[2 * w].T
         turned[2 * w + 1] = fetched[2 * w + 1].T
+
+    turn(HALF)
+    for n, w in enumerate(ask_near):
+        near(n, w, holder_of(w)).wait_recv()
+        turn(w)
+    for n, w in enumerate(ask_far):
+        rest = fetched.at[pl.ds(2 * w, 2), pl.ds(0, (TEAM - 1) * rows_far)]
+        remote(rest, rest, pass_send.at[n, 0], pass_recv.at[n], {"dom": me}).wait_recv()
+        turn(w)
+    pl.semaphore_wait(round_sem.at[2], 2)
 
     slot_copy.wait()
     tile_copy.wait()
@@ -165,25 +240,28 @@
 
     lax.fori_loop(0, ndom // 2, cut, 0)
 
+    def apart(k):
+        return ndom // 2 + (k >> 1) * (1 - 2 * (k & 1))
+
     def send_part(k, carry):
-        other = (me + k) & mask
-        remote(parts.at[other], came.at[me], sum_send, sum_recv, other).start()
+        other = (me + apart(k)) & mask
+        remote(parts.at[other], came.at[me], sum_send, sum_recv, {"dom": other}).start()
         return carry
 
     lax.fori_loop(1, ndom, send_part, 0)
     came[me] = parts[me]
     others = pl.ds(0, ndom - 1)
-    remote(came.at[others], came.at[others], sum_send, sum_recv, me).wait_recv()
+    remote(came.at[others], came.at[others], sum_send, sum_recv, {"dom": me}).wait_recv()
     summed = jnp.sum(came[...].astype(jnp.float32), axis=0)
     final[me] = summed.astype(jnp.bfloat16)
 
     def send_sum(k, carry):
-        other = (me + k) & mask
-        remote(final.at[me], final.at[me], all_send, all_recv, other).start()
+        other = (me + apart(k)) & mask
+        remote(final.at[me], final.at[me], all_send, all_recv, {"dom": other}).start()
         return carry
 
     lax.fori_loop(1, ndom, send_sum, 0)
-    remote(final.at[others], final.at[others], all_send, all_recv, me).wait_recv()
+    remote(final.at[others], final.at[others], all_send, all_recv, {"dom": me}).wait_recv()
 
     def put(g, carry):
         at = pl.ds(pl.multiple_of(g * 8, 8), 8)
@@ -193,11 +271,17 @@
 
     lax.fori_loop(0, ndom // 2, put, 0)
 
-    for w in ORDER:
-        remote(req_out.at[w], req_in.at[w], req_send.at[w], req_recv.at[w], holder_of(w)).wait_send()
-        remote(serve.at[w], fetched.at[pl.ds(2 * w, 2)], blk_send.at[w], blk_recv.at[w], asker_of(w)).wait_send()
-    remote(parts.at[others], parts.at[others], sum_send, sum_recv, me).wait_send()
-    remote(final.at[others], final.at[others], all_send, all_recv, me).wait_send()
+    for w in ask_far + ask_near:
+        request(w, holder_of(w)).wait_send()
+    for n, w in enumerate(serve_near):
+        near(n, w, asker_of(w)).wait_send()
+    for n, w in enumerate(serve_far):
+        far(n, w, asker_of(w)).wait_send()
+    for n, w in enumerate(ask_far):
+        for k in range(TEAM - 1):
+            pass_on(n, w, k).wait_send()
+    remote(parts.at[others], parts.at[others], sum_send, sum_recv, {"dom": me}).wait_send()
+    remote(final.at[others], final.at[others], all_send, all_recv, {"dom": me}).wait_send()
 
 
 def solution(mesh):
@@ -225,7 +309,8 @@
                 vmem((held, block, rank), bf16),
                 vmem((NEAR, 8, 128), i32),
                 vmem((NEAR, 8, 128), i32),
-                vmem((NEAR, 2, block, rank), bf16),
+                vmem((len(DIRECT) + 1, 2, block, rank), bf16),
+                vmem((2, 2, block // TEAM, rank), bf16),
                 vmem((2 * NEAR + 1, block, rank), bf16),
                 vmem((2 * NEAR, rank, block), bf16),
                 vmem((2, 128), i32),
@@ -239,8 +324,13 @@
                 dma,
                 dma((NEAR,)),
                 dma((NEAR,)),
-                dma((NEAR,)),
-                dma((NEAR,)),
+                dma((len(DIRECT) + 1,)),
+                dma((len(DIRECT) + 1,)),
+                dma((2,)),
+                dma((2,)),
+                dma((2, TEAM - 1)),
+                dma((2,)),
+                pltpu.SemaphoreType.REGULAR((3,)),
                 dma,
                 dma,
                 dma,

time: 58.1 us -> 57.8 us (level)
  no operation moved by 1% of the time
where the time goes in v2:
time: 57.8 us; the launch traced here: 57.6 us
  Pallas kernels  55.3 us (96%)
  local copies, waits for them, and re-layouts  1.67 us (3%)
  between operations  0.66 us (1%)
    pallas_call x1, Pallas kernels, on_device(): pl.pallas_call(functools.partial(kernel, ndom), out_shape=jax.ShapeDtypeS...  55.3 us
    unnamed x1, local copies, waits for them, and re-layouts  1.67 us

profile of v2, /device:TPU:1, one launch (start us, length us, event | category | flops | bytes accessed | tf_op | source)
XLA Modules:
  0.0 57.6 jit_solution(9967107359351701060)
XLA Ops:
  0.7 55.3 %shard_map.55 = f32[256,256]{1,0:T(8,128)} custom-call(s32[2,128]{1,0:T(2,128)} %bitcast.5, s32[4,128]{1,0:T(4,128)} %bitcast.4, s32[1]{0:T(128)S(6)} %copy.7.count_ref, bf16[128,128,128]{2,1,0:T(8,128)(2,1)} %tiles_hbm.1, bf16[8,128,256]{2,1,0:T(8,128)(2,1)} %bitcast.3), custom_call_target="tpu_custom_call" | custom-call | tf_op jit(solution)/shard_map/pallas_call | solution.py:296
  55.9 1.7 %copy.8 = f32[256,256]{1,0:T(8,128)} copy(f32[256,256]{1,0:T(8,128)} %shard_map.55) | data formatting | bytes 524288
